TPU v7x, 32 devices: a whole 2x2x4 slice. The times are simulated.
32 devices in a mesh: groups: 2 (over y), wide: 4 (over z), narrow: 4 (over x, core).
Axes of the slice: x: 2, y: 2, z: 4, core: 2. Of those that a mesh axis runs over, the one named last changes fastest.
Arguments:
- cont_queries: bfloat16 [32, 128, 64, 128], P(('groups', 'wide'), None, 'narrow'), parts along dimension 0, may hold values from -5 to 5
- cont_keys: bfloat16 [32, 128, 8, 128], P(('groups', 'wide'), None, 'narrow'), parts along dimension 0, may hold values from -5 to 5
- cont_values: bfloat16 [32, 128, 8, 128], P(('groups', 'wide'), None, 'narrow'), parts along dimension 0, may hold values from -5 to 5
- prefix_kv: bfloat16 [8, 2, 128, 8, 128], P(('groups', 'wide'), None, None, 'narrow'), parts along dimension 0, may hold values from -5 to 5
- probe: bfloat16 [64, 128], P('narrow'), may hold values from -0.5 to 0.5
- question_row: int32 [8], P('groups'), parts along dimension 0, may hold values from 0 to 3, each once
- cont_slot: int32 [32], P(('groups', 'wide')), parts along dimension 0, may hold values from 0 to 15, each once
- cont_length: int32 [32], P(('groups', 'wide')), parts along dimension 0, may hold values from 1 to 128
- gold: int32 [8], P('groups'), parts along dimension 0, may hold values from 0 to 3
Outputs:
- token_score: float32 [32, 128], P(('groups', 'wide')), parts along dimension 0
- owned_logprob: float32 [8, 4], P(('groups', 'wide')), parts along dimension 0
- owned_loss: float32 [8], P(('groups', 'wide')), parts along dimension 0
There are 2 independent parts, one for each index of `groups`. A program takes and returns all parts, laid end to end along the dimension named above; an argument that names none is the same for every part. Nothing has to cross between parts.
All inputs are finite; a program needn't handle non-finite values.
Results may differ from a plain program's by a relative error of at most 0.0065.
Values may be sent and summed in bfloat16 or wider, within the bound.
A program may use at most 64 MiB of HBM per device.

v0:
```python
import jax
import jax.numpy as jnp
from jax import lax
from jax.sharding import PartitionSpec as P

ANSWERS = 4


def attend_part(queries, keys, values, allowed, scale_factor):
    scores = (
        jnp.einsum("ctkgd,cjkd->ckgtj", queries, keys, preferred_element_type=jnp.float32)
        * scale_factor
    )
    scores = jnp.where(allowed[None, None, None, :, :], scores, -jnp.inf)
    row_max = jnp.max(scores, axis=-1)
    expo = jnp.exp(scores - row_max[..., None])
    total = jnp.sum(expo, axis=-1)
    weights = expo.astype(jnp.bfloat16)
    summed = jnp.einsum("ckgtj,cjkd->ctkgd", weights, values, preferred_element_type=jnp.float32)
    return (row_max, total, summed)


def to_rows(stat):
    return jnp.transpose(stat, (0, 3, 1, 2))[..., None]


def per_device(
    cont_queries,
    cont_keys,
    cont_values,
    prefix_kv,
    probe,
    question_row,
    cont_slot,
    cont_length,
    gold,
):
    cont_count, clen, heads_here, head_dim = cont_queries.shape
    kv_here = cont_keys.shape[2]
    group_size = heads_here // kv_here
    quest_here = prefix_kv.shape[0]
    pref_len = prefix_kv.shape[2]
    questions = question_row.shape[0]
    scale_factor = 1.0 / head_dim**0.5
    wanted = question_row[cont_slot // ANSWERS]
    piece = lax.all_gather(prefix_kv, "wide", axis=0, tiled=True)
    count = piece.shape[0]
    hits = (wanted[:, None] == jnp.arange(count, dtype=jnp.int32)[None, :]).astype(jnp.bfloat16)
    chosen = jnp.einsum("cn,nkpvd->ckpvd", hits, piece, preferred_element_type=jnp.float32)
    mine = chosen.astype(jnp.bfloat16)
    queries = cont_queries.reshape(cont_count, clen, kv_here, group_size, head_dim)
    causal = jnp.arange(clen)[:, None] >= jnp.arange(clen)[None, :]
    keys_all = jnp.concatenate([mine[:, 0], cont_keys], axis=1)
    values_all = jnp.concatenate([mine[:, 1], cont_values], axis=1)
    allowed = jnp.concatenate([jnp.ones((clen, pref_len), dtype=bool), causal], axis=1)
    row_max, total, summed = attend_part(queries, keys_all, values_all, allowed, scale_factor)
    output = summed / to_rows(total)
    attended = output.astype(jnp.bfloat16).reshape(cont_count, clen, heads_here, head_dim)
    partial_value = jnp.einsum("cthd,hd->ct", attended, probe, preferred_element_type=jnp.float32)
    token_score = lax.psum(partial_value, "narrow")
    valid = jnp.arange(clen)[None, :] < cont_length[:, None]
    choice_score = jnp.sum(jnp.where(valid, token_score, 0.0), axis=1)
    target = wanted * ANSWERS + cont_slot % ANSWERS
    spots = target[:, None] == jnp.arange(questions * ANSWERS, dtype=jnp.int32)[None, :]
    term = jnp.sum(jnp.where(spots, choice_score[:, None], 0.0), axis=0).reshape(questions, ANSWERS)
    first_row = lax.axis_index("wide") * quest_here
    totals = lax.psum(term, "wide")
    owned = lax.dynamic_slice_in_dim(totals, first_row, quest_here, 0)
    logprob = owned - jax.nn.logsumexp(owned, axis=1, keepdims=True)
    owned_rows = first_row + jnp.arange(quest_here, dtype=jnp.int32)
    matches = question_row[None, :] == owned_rows[:, None]
    gold_owned = jnp.sum(jnp.where(matches, gold[None, :], 0), axis=1)
    answer_ids = jnp.arange(ANSWERS, dtype=jnp.int32)[None, :]
    owned_loss = -jnp.sum(jnp.where(answer_ids == gold_owned[:, None], logprob, 0.0), axis=1)
    return (token_score, logprob, owned_loss)


def solution(mesh):
    return jax.shard_map(
        per_device,
        mesh=mesh,
        in_specs=(
            P(("groups", "wide"), None, "narrow", None),
            P(("groups", "wide"), None, "narrow", None),
            P(("groups", "wide"), None, "narrow", None),
            P(("groups", "wide"), None, None, "narrow", None),
            P("narrow", None),
            P("groups"),
            P(("groups", "wide")),
            P(("groups", "wide")),
            P("groups"),
        ),
        out_specs=(P(("groups", "wide"), None), P(("groups", "wide"), None), P(("groups", "wide"))),
        check_vma=False,
    )
```

profile of v0, /device:TPU:0, one launch (start us, length us, event | category | flops | bytes accessed | tf_op | source)
XLA Modules:
  0.0 57.5 jit_solution(3568872146050696365)
XLA Ops:
  0.6 0.0 copy-start
  0.6 0.8 %compare_select_fusion = s32[4]{0:T(128)S(1)} fusion(s32[4]{0:T(128)} %param.15), kind=kLoop, calls=%fused_computation.27 | loop fusion | flops 72 | bytes 32 | tf_op jit(solution)/shard_map/select_n | solution.py:45
  1.5 1.3 %gather_fusion = s32[4]{0:T(128)S(1)} fusion(s32[4]{0:T(128)} %param.14, s32[1024]{0:T(1024)S(1)} %pad_clamp_fusion), kind=kCustom, calls=%fused_computation | custom fusion | bytes 48 | tf_op jit(solution)/shard_map/gather | solution.py:45
  2.8 0.9 %copy.34 = bf16[1,2,128,2,128]{4,2,3,1,0:T(8,128)(2,1)S(1)} copy(bf16[1,2,128,2,128]{4,3,2,1,0:T(2,128)(2,1)} %param.12) | data formatting | bytes 262144 | tf_op args[3]
  3.7 17.4 %all_gather.3 = bf16[4,2,128,2,128]{4,2,3,1,0:T(8,128)(2,1)S(1)} all-gather(bf16[1,2,128,2,128]{4,2,3,1,0:T(8,128)(2,1)S(1)} %copy.34), channel_id=1, replica_groups=mesh['groups'=2,'wide'=4,'narrow'=4] {'wide'}, dimensions={0}, use_global_device_ids=true | all-gather | bytes 655360 | tf_op jit(solution)/shard_map/all_gather | solution.py:46
  21.1 0.5 convolution_convert_fusion
  21.6 0.2 slice_bitcast_fusion.1
  21.8 1.3 %copy.36 = bf16[4,128,2,128]{3,0,2,1:T(4,128)(2,1)S(1)} copy(bf16[4,128,2,128]{3,2,1,0:T(2,128)(2,1)} %param.11) | data formatting | bytes 524288 | tf_op args[2]
  23.1 1.3 %copy.37 = bf16[4,128,2,128]{3,0,2,1:T(4,128)(2,1)S(1)} copy(bf16[4,128,2,128]{3,2,1,0:T(2,128)(2,1)} %param.10) | data formatting | bytes 524288 | tf_op args[1]
  24.4 0.7 %maximum_bitcast_fusion = (bf16[4,256,2,128,1]{3,0,2,1,4:T(4,128)(2,1)S(1)}, bf16[4,256,2,128,1]{3,0,2,1,4:T(4,128)(2,1)S(1)}) fusion(bf16[4,128,2,128]{3,0,2,1:T(4,128)(2,1)S(1)} %copy.36, bf16[4,128,2,128]{3,0,2,1:T(4,128)(2,1)S(1)} %get-tuple-element.5, bf16[4,128,2,128]{3,0,2,1:T(4,128)(2,1)S(1)} %copy.37, bf16[4,128,2,128]{3,0,2,1:T(4,128)(2,1)S(1)} %get-tuple-element.6), kind=kLoop, calls=%fused_computation.16 | loop fusion | flops 524288 | bytes 2097152 | tf_op jit(solution)/shard_map/concatenate | solution.py:54
  25.1 1.5 %fusion.2 = (f32[4,2,8,128]{3,2,1,0:T(8,128)S(1)}, f32[4,2,256,128,8]{3,2,4,1,0:T(8,128)S(1)}) fusion(pred[128,256]{0,1:T(8,128)(4,1)S(1)} %concatenate.10, bf16[4,128,2,8,128]{4,3,2,1,0:T(8,128)(2,1)S(1)} %bitcast.41, bf16[4,256,2,128,1]{3,0,2,1,4:T(4,128)(2,1)S(1)} %get-tuple-element.10), kind=kOutput, calls=%fused_computation.5 | convolution fusion | flops 543154176 | bytes 11075584 | tf_op jit(solution)/shard_map/ctkgd,cjkd->ckgtj/dot_general | solution.py:11
  26.7 2.2 %fusion = f32[4,2,8,128]{3,2,1,0:T(8,128)S(1)} fusion(f32[4,2,256,128,8]{3,2,4,1,0:T(8,128)S(1)} %get-tuple-element.8, f32[4,2,8,128]{3,2,1,0:T(8,128)S(1)} %get-tuple-element.7, pred[128,256]{0,1:T(8,128)(4,1)S(1)} %concatenate.10), kind=kLoop, calls=%fused_computation.3 | loop fusion | flops 8380416 | bytes 8486912 | tf_op jit(solution)/shard_map/reduce_sum | solution.py:17
  28.9 0.0 copy-start.4
  29.0 2.4 %fusion.5 = bf16[4,128,2,8,128]{1,4,3,2,0:T(8,128)(2,1)S(1)} fusion(f32[4,128,2,8]{1,3,2,0:T(8,128)S(1)} %bitcast.43, f32[4,2,256,128,8]{3,2,4,1,0:T(8,128)S(1)} %get-tuple-element.8, f32[4,2,8,128]{3,2,1,0:T(8,128)S(1)} %get-tuple-element.7, pred[128,256]{0,1:T(8,128)(4,1)S(1)} %concatenate.10, bf16[4,256,2,128,1]{3,0,2,1,4:T(4,128)(2,1)S(1)} %get-tuple-element.9), kind=kOutput, calls=%fused_computation.8 | convolution fusion | flops 547356672 | bytes 11108352 | tf_op jit(solution)/shard_map/ckgtj,cjkd->ctkgd/dot_general | solution.py:19
  31.3 0.4 fusion.17
  31.7 5.6 %psum.14 = f32[4,128]{1,0:T(4,128)S(1)} all-reduce(f32[4,128]{1,0:T(4,128)S(1)} %bitcast.45), channel_id=1, replica_groups=mesh['groups'=2,'wide'=4,'narrow'=4] {'narrow'}, use_global_device_ids=true, to_apply=%region_2.3 | all-reduce | flops 512 | bytes 4096 | tf_op jit(solution)/shard_map/psum | solution.py:60
  37.4 0.2 select_reduce_fusion.1
  37.6 0.1 select_reduce_fusion
  37.7 0.1 reshape.54
  37.7 12.5 %psum.15 = f32[4,4]{1,0:T(4,128)S(1)} all-reduce(f32[4,4]{1,0:T(4,128)S(1)} %reshape.54), channel_id=1, replica_groups=mesh['groups'=2,'wide'=4,'narrow'=4] {'wide'}, use_global_device_ids=true, to_apply=%region_5.6 | all-reduce | flops 16 | bytes 128 | tf_op jit(solution)/shard_map/psum | solution.py:67
  50.2 0.6 %fusion.27 = f32[]{:T(128)} fusion(f32[4,4]{1,0:T(4,128)S(1)} %psum.15, s32[]{:T(128)S(6)} %select_n.48), kind=kLoop, calls=%fused_computation.50 | loop fusion | flops 3 | bytes 24 | tf_op jit(solution)/shard_map/reduce_max | solution.py:69
  52.1 0.6 %exponential_reduce_fusion = f32[]{:T(128)} fusion(f32[]{:T(128)} %bitcast.15, f32[4,4]{1,0:T(4,128)S(1)} %psum.15, s32[]{:T(128)S(6)} %select_n.48), kind=kLoop, calls=%fused_computation.45 | loop fusion | flops 7 | bytes 28 | tf_op jit(solution)/shard_map/reduce_sum | solution.py:69
  53.4 0.6 %fusion.23 = s32[]{:T(128)} fusion(s32[4]{0:T(128)S(1)} %copy-done.5, s32[4]{0:T(128)S(1)} %copy-done.1, s32[]{:T(128)S(6)} %axis_index.15), kind=kLoop, calls=%fused_computation.43 | loop fusion | flops 11 | bytes 40 | tf_op jit(solution)/shard_map/reduce_sum | solution.py:72
  54.1 1.8 %fusion.24 = (f32[]{:T(128)}, f32[1,4]{1,0:T(1,128)}) fusion(s32[]{:T(128)} %fusion.23, f32[]{:T(128)} %bitcast.17, f32[4,4]{1,0:T(4,128)S(1)} %psum.15, s32[]{:T(128)S(6)} %select_n.48), kind=kLoop, calls=%fused_computation.44 | loop fusion | flops 15 | bytes 48 | tf_op jit(solution)/shard_map/reduce_sum | solution.py:74
  (16 shorter events, 0.1 us)
Async XLA Ops:
  0.6 24.5 %copy-start = (bf16[4,128,16,128]{3,2,1,0:T(8,128)(2,1)S(1)}, bf16[4,128,16,128]{3,2,1,0:T(8,128)(2,1)}, u32[]{:S(2)}) copy-start(bf16[4,128,16,128]{3,2,1,0:T(8,128)(2,1)} %param.9) | copy-start | bytes 6291460
  28.9 2.4 %copy-start.2 = (bf16[16,128]{1,0:T(8,128)(2,1)S(1)}, bf16[16,128]{1,0:T(8,128)(2,1)}, u32[]{:S(2)}) copy-start(bf16[16,128]{1,0:T(8,128)(2,1)} %param.13) | copy-start | bytes 12292
  28.9 8.4 %copy-start.4 = (s32[4]{0:T(128)S(1)}, s32[4]{0:T(128)}, u32[]{:S(2)}) copy-start(s32[4]{0:T(128)} %param.16) | copy-start | bytes 52
  28.9 8.6 %copy-start.6 = (s32[4]{0:T(128)S(1)}, s32[4]{0:T(128)}, u32[]{:S(2)}) copy-start(s32[4]{0:T(128)} %param.15) | copy-start | bytes 52
  29.0 24.5 %copy-start.1 = (s32[4]{0:T(128)S(1)}, s32[4]{0:T(128)}, u32[]{:S(2)}) copy-start(s32[4]{0:T(128)} %param.14) | copy-start | bytes 52
  29.0 24.5 %copy-start.5 = (s32[4]{0:T(128)S(1)}, s32[4]{0:T(128)}, u32[]{:S(2)}) copy-start(s32[4]{0:T(128)} %param.17) | copy-start | bytes 52
  37.4 19.0 %copy-start.3 = (f32[4,128]{1,0:T(4,128)}, f32[4,128]{1,0:T(4,128)S(1)}, u32[]{:S(2)}) copy-start(f32[4,128]{1,0:T(4,128)S(1)} %psum.14) | copy-start | bytes 6148
where the time goes:
time: 57.8 us; the launch traced here: 57.5 us
  blocking collectives  35.5 us (61%)
  other arithmetic  7.63 us (13%)
  local copies, waits for them, and re-layouts  5.13 us (9%)
  matrix products  4.82 us (8%)
  between operations  4.47 us (8%)
    all_gather x1, blocking collectives, per_device(): piece = lax.all_gather(prefix_kv, 'wide', axis=0, tiled=True)  17.4 us
    psum x1, blocking collectives, per_device(): totals = lax.psum(term, 'wide')  12.5 us
    psum x1, blocking collectives, per_device(): token_score = lax.psum(partial_value, 'narrow')  5.64 us
    unnamed x17, local copies, waits for them, and re-layouts  3.56 us
    dot_general x1, matrix products, attend_part(): jnp.einsum('ckgtj,cjkd->ctkgd', weights, values, preferred_element_type=j...  2.35 us
    reduce_sum x1, other arithmetic, attend_part(): total = jnp.sum(expo, axis=-1)  2.23 us
    reduce_sum x1, other arithmetic, per_device(): jnp.sum(jnp.where(answer_ids == gold_owned[:, None], logprob, 0.0), axis=1)  1.75 us
    dot_general x1, matrix products, attend_part(): jnp.einsum('ctkgd,cjkd->ckgtj', queries, keys, preferred_element_type=jnp...  1.54 us

commit v1 on v0

v1 whole, which is shorter than its diff:
```python
import functools

import jax
import jax.numpy as jnp
from jax import lax
from jax.experimental import pallas as pl
from jax.experimental.pallas import tpu as pltpu
from jax.sharding import PartitionSpec as P

MESH = pl.DeviceIdType.MESH
ANSWERS = 4
LANES = 128
NEG = -1e30
LOG2E = 1.4426950408889634
F32 = jnp.float32
BF16 = jnp.bfloat16
NT = (((1,), (1,)), ((), ()))
TN = (((0,), (0,)), ((), ()))


def iota(shape, dim):
    return lax.broadcasted_iota(jnp.int32, shape, dim)


def kernel(
    sizes,
    qrow_ref, slot_ref, len_ref, gold_ref, q_hbm, k_hbm, v_hbm, pre_hbm, probe_ref,
    tok_ref, logp_ref, loss_ref,
    q_v, k_v, v_v, pv_v, kslot, vpslot, split, kown, vpt, kpre, vptp,
    m1, l1, n1, m2, l2, n2, tslot, cbuf, cslot,
    in_sem, ksend, krecv, vsend, vrecv, tsend, trecv, csend, crecv,
):
    wide, narrow, conts, clen, heads, kv, dim, quest, pref, questions = sizes
    group = heads // kv
    scale = LOG2E / dim**0.5
    me_w = lax.axis_index("wide")
    me_n = lax.axis_index("narrow")
    tcols = 2 * LANES // heads
    cols = tcols * heads
    blocks = clen // tcols
    own = pl.ds(me_w * quest, quest)

    cp_k = pltpu.make_async_copy(pre_hbm.at[:, 0], kslot.at[own], in_sem.at[0])
    cp_v = pltpu.make_async_copy(pre_hbm.at[:, 1], pv_v, in_sem.at[1])
    cp_ko = pltpu.make_async_copy(k_hbm, k_v, in_sem.at[2])
    cp_vo = pltpu.make_async_copy(v_hbm, v_v, in_sem.at[3])
    cp_q = pltpu.make_async_copy(q_hbm, q_v, in_sem.at[4])
    for cp in (cp_k, cp_v, cp_ko, cp_vo, cp_q):
        cp.start()

    barrier = pltpu.get_barrier_semaphore()
    total = wide * narrow
    me = me_w * narrow + me_n

    def peer(i):
        p = lax.rem(me + i, total)
        return {"wide": lax.div(p, narrow), "narrow": lax.rem(p, narrow)}

    def greet(i, _):
        pl.semaphore_signal(barrier, inc=1, device_id=peer(i), device_id_type=MESH)
        return 0

    lax.fori_loop(1, total, greet, 0)

    probe = probe_ref[...]
    lane = iota((1, LANES), 1)
    lane_kv = (lane % heads) // group
    rowsel = iota((LANES, heads), 0) % heads == iota((LANES, heads), 1)
    tile_mat = jnp.where(rowsel, 1.0, 0.0).astype(BF16)
    probe_t = lax.dot_general(
        tile_mat, probe, (((1,), (0,)), ((), ())), preferred_element_type=F32
    ).astype(BF16)
    expand = jnp.where(iota((heads, LANES), 1) % heads == iota((heads, LANES), 0), 1.0, 0.0)

    def unpack(x):
        split[...] = x.astype(F32)
        n = x.shape[0] // kv
        return [split[pl.ds(i, n, stride=kv), :] for i in range(kv)]

    cp_v.wait()
    head_kv = iota((heads, 1), 0) // group
    for r in range(quest):
        acc = jnp.zeros((heads, pref), F32)
        for i, part in enumerate(unpack(pv_v[r])):
            d = lax.dot_general(probe, part.astype(BF16), NT, preferred_element_type=F32)
            acc = jnp.where(head_kv == i, d, acc)
        vpslot[me_w * quest + r] = acc
    cp_k.wait()
    pl.semaphore_wait(barrier, total - 1)

    def wpeer(i):
        return lax.rem(me_w + i, wide)

    def kcopy(i):
        return pltpu.make_async_remote_copy(
            src_ref=kslot.at[own], dst_ref=kslot.at[own],
            send_sem=ksend.at[i - 1], recv_sem=krecv.at[i - 1],
            device_id={"wide": wpeer(i)}, device_id_type=MESH,
        )

    def vcopy(i):
        return pltpu.make_async_remote_copy(
            src_ref=vpslot.at[own], dst_ref=vpslot.at[own],
            send_sem=vsend.at[i - 1], recv_sem=vrecv.at[i - 1],
            device_id={"wide": wpeer(i)}, device_id_type=MESH,
        )

    def each_peer(count, fn):
        def step(i, _):
            fn(i)
            return 0
        lax.fori_loop(1, count, step, 0)

    each_peer(wide, lambda i: kcopy(i).start())
    each_peer(wide, lambda i: vcopy(i).start())

    def start_mask(c, b):
        rows = q_v[c, pl.ds(b * cols, cols), :]
        rk = (iota((cols, 1), 0) % heads) // group
        return jnp.concatenate(
            [rows * jnp.where(rk == i, 1.0, 0.0).astype(BF16) for i in range(kv)], axis=1
        )

    def softmax_part(s, vp):
        m = jnp.max(s, axis=0, keepdims=True)
        e = jnp.exp2((s - m) * scale)
        l = jnp.sum(e, axis=0, keepdims=True)
        n = jnp.sum(e * jnp.concatenate([vp] * (cols // LANES), axis=1), axis=0, keepdims=True)
        return m, l, n

    cp_ko.wait()
    cp_vo.wait()
    cp_q.wait()

    def own_part(c, _):
        parts = unpack(k_v[c])
        for i in range(kv):
            kown[:, i * dim:(i + 1) * dim] = parts[i].astype(BF16)
        d = lax.dot_general(v_v[c], probe_t, NT, preferred_element_type=F32)
        split[...] = d
        acc = split[pl.ds(0, clen, stride=kv), :]
        for i in range(1, kv):
            acc = jnp.where(lane_kv == i, split[pl.ds(i, clen, stride=kv), :], acc)
        vpt[...] = acc
        for b in range(blocks):
            n_rows = (b + 1) * tcols
            q2 = start_mask(c, b)
            s = lax.dot_general(kown[:n_rows, :], q2, NT, preferred_element_type=F32)
            ok = iota((tcols, cols), 0) <= iota((tcols, cols), 1) // heads
            last = jnp.where(ok, s[n_rows - tcols:], NEG)
            s = last if b == 0 else jnp.concatenate([s[:n_rows - tcols], last], axis=0)
            m, l, n = softmax_part(s, vpt[:n_rows, :])
            m1[c, b:b + 1, :] = m
            l1[c, b:b + 1, :] = l
            n1[c, b:b + 1, :] = n
        return 0

    lax.fori_loop(0, conts, own_part, 0)

    each_peer(wide, lambda i: kcopy(i).wait())
    each_peer(wide, lambda i: vcopy(i).wait())

    def prefix_part(c, _):
        w = qrow_ref[slot_ref[c] // ANSWERS]
        parts = unpack(kslot[w])
        for i in range(kv):
            kpre[:, i * dim:(i + 1) * dim] = parts[i].astype(BF16)
        vptp[...] = lax.dot_general(
            vpslot[w], expand, TN, preferred_element_type=F32, precision=lax.Precision.HIGHEST
        )
        for b in range(blocks):
            q2 = start_mask(c, b)
            s = lax.dot_general(kpre[...], q2, NT, preferred_element_type=F32)
            m, l, n = softmax_part(s, vptp[...])
            m2[c, b:b + 1, :] = m
            l2[c, b:b + 1, :] = l
            n2[c, b:b + 1, :] = n
        return 0

    lax.fori_loop(0, conts, prefix_part, 0)

    fold = jnp.where(iota((cols, clen), 0) // heads == iota((cols, clen), 1) % tcols, 1.0, 0.0)
    keep = iota((blocks, clen), 1) // tcols == iota((blocks, clen), 0)
    row_id = iota((conts, clen), 0)
    partial = jnp.zeros((conts, clen), F32)
    for c in range(conts):
        ma, mb = m1[c], m2[c]
        m = jnp.maximum(ma, mb)
        ea, eb = jnp.exp2((ma - m) * scale), jnp.exp2((mb - m) * scale)
        ratio = (n1[c] * ea + n2[c] * eb) / (l1[c] * ea + l2[c] * eb)
        y = jnp.dot(ratio, fold, preferred_element_type=F32, precision=lax.Precision.HIGHEST)
        y = jnp.sum(jnp.where(keep, y, 0.0), axis=0, keepdims=True)
        partial = jnp.where(row_id == c, y, partial)
    tslot[me_n] = partial

    choice_rows = wide * quest
    crow = iota((wide, quest, LANES), 0) * quest + iota((wide, quest, LANES), 1)
    clane = iota((wide, quest, LANES), 2)
    term = jnp.zeros((wide, quest, LANES), F32)
    tpos = iota((1, clen), 1)
    for c in range(conts):
        slot = slot_ref[c]
        w = qrow_ref[slot // ANSWERS]
        a = slot % ANSWERS
        val = jnp.sum(jnp.where(tpos < len_ref[c], partial[c:c + 1, :], 0.0), axis=1, keepdims=True)
        term = term + jnp.where((crow == w) & (clane == a), val.reshape(1, 1, 1), 0.0)
    cbuf[...] = term

    def tcopy(i):
        return pltpu.make_async_remote_copy(
            src_ref=tslot.at[me_n], dst_ref=tslot.at[me_n],
            send_sem=tsend.at[i - 1], recv_sem=trecv.at[i - 1],
            device_id={"narrow": lax.rem(me_n + i, narrow)}, device_id_type=MESH,
        )

    def ccopy(i):
        to = peer(i)
        return pltpu.make_async_remote_copy(
            src_ref=cbuf.at[to["wide"]], dst_ref=cslot.at[me],
            send_sem=csend.at[i - 1], recv_sem=crecv.at[i - 1],
            device_id=to, device_id_type=MESH,
        )

    each_peer(total, lambda i: ccopy(i).start())
    each_peer(narrow, lambda i: tcopy(i).start())
    cslot[me] = cbuf[me_w]

    each_peer(narrow, lambda i: tcopy(i).wait())
    tok = tslot[0]
    for i in range(1, narrow):
        tok = tok + tslot[i]
    tok_ref[...] = tok

    each_peer(total, lambda i: ccopy(i).wait())
    scores = jnp.sum(cslot[...], axis=0)
    live = iota((quest, LANES), 1) < ANSWERS
    masked = jnp.where(live, scores, NEG)
    top = jnp.max(masked, axis=1, keepdims=True)
    norm = jnp.log(jnp.sum(jnp.where(live, jnp.exp(masked - top), 0.0), axis=1, keepdims=True))
    logp = scores - top - norm
    logp_ref[...] = logp[:, :ANSWERS]
    mine = me_w * quest + iota((quest, 1), 0)
    gold = jnp.zeros((quest, 1), jnp.int32)
    for g in range(questions):
        gold = jnp.where(mine == qrow_ref[g], gold_ref[g], gold)
    pick = iota((quest, LANES), 1) == gold
    loss_ref[...] = -jnp.sum(jnp.where(pick, logp, 0.0), axis=1, keepdims=True)


def solution(mesh):
    wide, narrow = mesh.shape["wide"], mesh.shape["narrow"]
    total = wide * narrow

    def per_device(q, k, v, prefix, probe, qrow, slot, length, gold):
        conts, clen, heads, dim = q.shape
        kv = k.shape[2]
        quest, _, pref = prefix.shape[:3]
        questions = qrow.shape[0]
        cols = 2 * LANES // heads * heads
        blocks = clen * heads // cols
        sizes = (wide, narrow, conts, clen, heads, kv, dim, quest, pref, questions)
        smem = pl.BlockSpec(memory_space=pltpu.SMEM)
        vmem = pl.BlockSpec(memory_space=pltpu.VMEM)
        anyw = pl.BlockSpec(memory_space=pl.ANY)
        stat = pltpu.VMEM((conts, blocks, cols), F32)
        dma = pltpu.SemaphoreType.DMA
        tok, logp, loss = pl.pallas_call(
            functools.partial(kernel, sizes),
            out_shape=(
                jax.ShapeDtypeStruct((conts, clen), F32),
                jax.ShapeDtypeStruct((quest, ANSWERS), F32),
                jax.ShapeDtypeStruct((quest, 1), F32),
            ),
            in_specs=[smem] * 4 + [anyw] * 4 + [vmem],
            out_specs=(vmem, vmem, vmem),
            scratch_shapes=[
                pltpu.VMEM((conts, clen * heads, dim), BF16),
                pltpu.VMEM((conts, clen * kv, dim), BF16),
                pltpu.VMEM((conts, clen * kv, dim), BF16),
                pltpu.VMEM((quest, pref * kv, dim), BF16),
                pltpu.VMEM((wide * quest, pref * kv, dim), BF16),
                pltpu.VMEM((wide * quest, heads, pref), F32),
                pltpu.VMEM((clen * kv, dim), F32),
                pltpu.VMEM((clen, kv * dim), BF16),
                pltpu.VMEM((clen, LANES), F32),
                pltpu.VMEM((pref, kv * dim), BF16),
                pltpu.VMEM((pref, LANES), F32),
                stat, stat, stat, stat, stat, stat,
                pltpu.VMEM((narrow, conts, clen), F32),
                pltpu.VMEM((wide, quest, LANES), F32),
                pltpu.VMEM((total, quest, LANES), F32),
                dma((5,)),
                dma((wide - 1,)), dma((wide - 1,)), dma((wide - 1,)), dma((wide - 1,)),
                dma((narrow - 1,)), dma((narrow - 1,)), dma((total - 1,)), dma((total - 1,)),
            ],
            compiler_params=pltpu.CompilerParams(collective_id=0, has_side_effects=True),
        )(
            qrow, slot, length, gold,
            q.reshape(conts, clen * heads, dim),
            k.reshape(conts, clen * kv, dim),
            v.reshape(conts, clen * kv, dim),
            prefix.reshape(quest, 2, pref * kv, dim),
            probe,
        )
        return tok, logp, loss.reshape(quest)

    return jax.shard_map(
        per_device,
        mesh=mesh,
        in_specs=(
            P(("groups", "wide"), None, "narrow", None),
            P(("groups", "wide"), None, "narrow", None),
            P(("groups", "wide"), None, "narrow", None),
            P(("groups", "wide"), None, None, "narrow", None),
            P("narrow", None),
            P("groups"),
            P(("groups", "wide")),
            P(("groups", "wide")),
            P("groups"),
        ),
        out_specs=(P(("groups", "wide"), None), P(("groups", "wide"), None), P(("groups", "wide"))),
        check_vma=False,
    )
```

time: 57.8 us -> 28.3 us (0.49)
  blocking collectives: 35.5 us -> 0 us
  Pallas kernels: 0 us -> 23.3 us
  other arithmetic: 7.63 us -> 0 us
  matrix products: 4.82 us -> 0 us
  local copies, waits for them, and re-layouts: 5.13 us -> 2.39 us
  between operations: 4.47 us -> 2.4 us
    pallas_call x0 -> x1, Pallas kernels: none -> 23.3 us  [per_device(): pl.pallas_call(functools.partial(kernel, sizes), out_shape=(jax.ShapeDtyp...]
    psum x2 -> x0, blocking collectives: 18.1 us -> none  [the longest x1 12.5 us: per_device(): totals = lax.psum(term, 'wide')]
    all_gather x1 -> x0, blocking collectives: 17.4 us -> none  [per_device(): piece = lax.all_gather(prefix_kv, 'wide', axis=0, tiled=True)]
    reduce_sum x6 -> x0, other arithmetic: 5.49 us -> none  [the longest x1 2.23 us: attend_part(): total = jnp.sum(expo, axis=-1)]
    dot_general x4 -> x0, matrix products: 4.82 us -> none  [the longest x1 2.35 us: attend_part(): jnp.einsum('ckgtj,cjkd->ctkgd', weights, values, preferred_element_type=j...]
    gather x1 -> x0, local copies, waits for them, and re-layouts: 1.29 us -> none  [per_device(): wanted = question_row[cont_slot // ANSWERS]]
    unnamed x17 -> x2, local copies, waits for them, and re-layouts: 3.56 us -> 2.39 us
    select_n x1 -> x0, other arithmetic: 0.82 us -> none  [per_device(): wanted = question_row[cont_slot // ANSWERS]]
where the time goes in v1:
time: 28.3 us; the launch traced here: 28.1 us
  Pallas kernels  23.3 us (82%)
  between operations  2.4 us (8%)
  local copies, waits for them, and re-layouts  2.39 us (8%)
    pallas_call x1, Pallas kernels, per_device(): pl.pallas_call(functools.partial(kernel, sizes), out_shape=(jax.ShapeDtyp...  23.3 us
    unnamed x2, local copies, waits for them, and re-layouts  2.39 us

profile of v1, /device:TPU:0, one launch (start us, length us, event | category | flops | bytes accessed | tf_op | source)
XLA Modules:
  0.0 28.1 jit_solution(12213814090243187571)
XLA Ops:
  0.6 23.3 %shard_map.112 = (f32[4,128]{1,0:T(4,128)}, f32[1,4]{1,0:T(1,128)}, f32[1,1]{1,0:T(1,128)}) custom-call(s32[4]{0:T(128)} %qrow_ref.1, s32[4]{0:T(128)} %slot_ref.1, s32[4]{0:T(128)} %len_ref.1, s32[4]{0:T(128)} %gold_ref.1, bf16[4,2048,128]{2,1,0:T(8,128)(2,1)} %bitcast.5, bf16[4,256,128]{2,1,0:T(8,128)(2,1)} %bitcast.6, bf16[4,256,128]{2,1,0:T(8,128)(2,1)} %bitcast.7, ...), custom_call_target="tpu_custom_call" | custom-call | tf_op jit(solution)/shard_map/pallas_call | solution.py:267
  23.9 1.2 %copy.15 = f32[4,128]{1,0:T(4,128)} copy(f32[4,128]{1,0:T(4,128)} %get-tuple-element.12) | data formatting | bytes 4096
  25.2 1.1 %copy.16 = f32[1,4]{1,0:T(1,128)} copy(f32[1,4]{1,0:T(1,128)} %get-tuple-element.13) | data formatting | bytes 32

commit v2 on v1

--- a/solution.py
+++ b/solution.py
@@ -25,7 +25,7 @@
 def kernel(
     sizes,
     qrow_ref, slot_ref, len_ref, gold_ref, q_hbm, k_hbm, v_hbm, pre_hbm, probe_ref,
-    tok_ref, logp_ref, loss_ref,
+    out_ref,
     q_v, k_v, v_v, pv_v, kslot, vpslot, split, kown, vpt, kpre, vptp,
     m1, l1, n1, m2, l2, n2, tslot, cbuf, cslot,
     in_sem, ksend, krecv, vsend, vrecv, tsend, trecv, csend, crecv,
@@ -48,19 +48,19 @@
     for cp in (cp_k, cp_v, cp_ko, cp_vo, cp_q):
         cp.start()
 
-    barrier = pltpu.get_barrier_semaphore()
     total = wide * narrow
     me = me_w * narrow + me_n
+    right, left = lax.rem(me_w + 1, wide), lax.rem(me_w + wide - 1, wide)
 
     def peer(i):
         p = lax.rem(me + i, total)
         return {"wide": lax.div(p, narrow), "narrow": lax.rem(p, narrow)}
 
-    def greet(i, _):
-        pl.semaphore_signal(barrier, inc=1, device_id=peer(i), device_id_type=MESH)
-        return 0
-
-    lax.fori_loop(1, total, greet, 0)
+    barrier = pltpu.get_barrier_semaphore()
+    near = [{"wide": right}, {"wide": left}]
+    near += [{"narrow": lax.rem(me_n + i, narrow)} for i in range(1, narrow)]
+    for to in near:
+        pl.semaphore_signal(barrier, inc=1, device_id=to, device_id_type=MESH)
 
     probe = probe_ref[...]
     lane = iota((1, LANES), 1)
@@ -86,33 +86,38 @@
             acc = jnp.where(head_kv == i, d, acc)
         vpslot[me_w * quest + r] = acc
     cp_k.wait()
-    pl.semaphore_wait(barrier, total - 1)
-
-    def wpeer(i):
-        return lax.rem(me_w + i, wide)
-
-    def kcopy(i):
+    pl.semaphore_wait(barrier, len(near))
+
+    steps = wide // 2
+
+    def ring_copy(buf, sends, recvs, step, way, half):
+        size = buf.shape[1] // 2
+        row = lax.rem(me_w + (wide - step + 1 if way == 0 else step - 1), wide)
+        part = buf.at[pl.ds(row * quest, quest), pl.ds(half * size, size)]
+        n = ((step - 1) * 2 + way) * 2 + half
         return pltpu.make_async_remote_copy(
-            src_ref=kslot.at[own], dst_ref=kslot.at[own],
-            send_sem=ksend.at[i - 1], recv_sem=krecv.at[i - 1],
-            device_id={"wide": wpeer(i)}, device_id_type=MESH,
-        )
-
-    def vcopy(i):
-        return pltpu.make_async_remote_copy(
-            src_ref=vpslot.at[own], dst_ref=vpslot.at[own],
-            send_sem=vsend.at[i - 1], recv_sem=vrecv.at[i - 1],
-            device_id={"wide": wpeer(i)}, device_id_type=MESH,
-        )
+            src_ref=part, dst_ref=part, send_sem=sends.at[n], recv_sem=recvs.at[n],
+            device_id={"wide": right if way == 0 else left}, device_id_type=MESH,
+        )
+
+    def ring_step(step):
+        out = []
+        for turn in range(2 if step < steps else 1):
+            for way in range(2):
+                half = way if turn == 0 else 1 - way
+                for args in ((vpslot, vsend, vrecv), (kslot, ksend, krecv)):
+                    out.append(ring_copy(*args, step, way, half))
+        return out
+
+    pending = ring_step(1)
+    for cp in pending:
+        cp.start()
 
     def each_peer(count, fn):
         def step(i, _):
             fn(i)
             return 0
         lax.fori_loop(1, count, step, 0)
-
-    each_peer(wide, lambda i: kcopy(i).start())
-    each_peer(wide, lambda i: vcopy(i).start())
 
     def start_mask(c, b):
         rows = q_v[c, pl.ds(b * cols, cols), :]
@@ -157,8 +162,24 @@
 
     lax.fori_loop(0, conts, own_part, 0)
 
-    each_peer(wide, lambda i: kcopy(i).wait())
-    each_peer(wide, lambda i: vcopy(i).wait())
+    sent = list(pending)
+    for step in range(2, steps + 1):
+        later = ring_step(step)
+        lead = len(later) if step == steps else 0
+        for got, cp in zip(pending[:lead], later[:lead]):
+            got.wait_recv()
+            cp.start()
+        for got in pending[lead:]:
+            got.wait_recv()
+        if lead == 0:
+            for cp in later:
+                cp.start()
+        sent += later
+        pending = later
+    for cp in pending:
+        cp.wait_recv()
+    for cp in sent:
+        cp.wait_send()
 
     def prefix_part(c, _):
         w = qrow_ref[slot_ref[c] // ANSWERS]
@@ -229,7 +250,7 @@
     tok = tslot[0]
     for i in range(1, narrow):
         tok = tok + tslot[i]
-    tok_ref[...] = tok
+    out_ref[0:conts, :] = tok
 
     each_peer(total, lambda i: ccopy(i).wait())
     scores = jnp.sum(cslot[...], axis=0)
@@ -238,13 +259,20 @@
     top = jnp.max(masked, axis=1, keepdims=True)
     norm = jnp.log(jnp.sum(jnp.where(live, jnp.exp(masked - top), 0.0), axis=1, keepdims=True))
     logp = scores - top - norm
-    logp_ref[...] = logp[:, :ANSWERS]
+    out_ref[conts:conts + quest, :] = logp
     mine = me_w * quest + iota((quest, 1), 0)
     gold = jnp.zeros((quest, 1), jnp.int32)
     for g in range(questions):
         gold = jnp.where(mine == qrow_ref[g], gold_ref[g], gold)
     pick = iota((quest, LANES), 1) == gold
-    loss_ref[...] = -jnp.sum(jnp.where(pick, logp, 0.0), axis=1, keepdims=True)
+    loss = -jnp.sum(jnp.where(pick, logp, 0.0), axis=1, keepdims=True)
+    out_ref[conts + quest:conts + 2 * quest, :] = jnp.broadcast_to(loss, (quest, LANES))
+
+
+def hand_out(conts, quest, packed_ref, tok_ref, logp_ref, loss_ref):
+    tok_ref[...] = packed_ref[0:conts, :]
+    logp_ref[...] = packed_ref[conts:conts + quest, :ANSWERS]
+    loss_ref[...] = packed_ref[conts + quest:conts + 2 * quest, :1]
 
 
 def solution(mesh):
@@ -264,15 +292,11 @@
         anyw = pl.BlockSpec(memory_space=pl.ANY)
         stat = pltpu.VMEM((conts, blocks, cols), F32)
         dma = pltpu.SemaphoreType.DMA
-        tok, logp, loss = pl.pallas_call(
+        packed = pl.pallas_call(
             functools.partial(kernel, sizes),
-            out_shape=(
-                jax.ShapeDtypeStruct((conts, clen), F32),
-                jax.ShapeDtypeStruct((quest, ANSWERS), F32),
-                jax.ShapeDtypeStruct((quest, 1), F32),
-            ),
+            out_shape=jax.ShapeDtypeStruct((conts + 2 * quest, LANES), F32),
             in_specs=[smem] * 4 + [anyw] * 4 + [vmem],
-            out_specs=(vmem, vmem, vmem),
+            out_specs=vmem,
             scratch_shapes=[
                 pltpu.VMEM((conts, clen * heads, dim), BF16),
                 pltpu.VMEM((conts, clen * kv, dim), BF16),
@@ -290,7 +314,7 @@
                 pltpu.VMEM((wide, quest, LANES), F32),
                 pltpu.VMEM((total, quest, LANES), F32),
                 dma((5,)),
-                dma((wide - 1,)), dma((wide - 1,)), dma((wide - 1,)), dma((wide - 1,)),
+                dma((2 * wide,)), dma((2 * wide,)), dma((2 * wide,)), dma((2 * wide,)),
                 dma((narrow - 1,)), dma((narrow - 1,)), dma((total - 1,)), dma((total - 1,)),
             ],
             compiler_params=pltpu.CompilerParams(collective_id=0, has_side_effects=True),
@@ -302,6 +326,16 @@
             prefix.reshape(quest, 2, pref * kv, dim),
             probe,
         )
+        tok, logp, loss = pl.pallas_call(
+            functools.partial(hand_out, conts, quest),
+            out_shape=(
+                jax.ShapeDtypeStruct((conts, clen), F32),
+                jax.ShapeDtypeStruct((quest, ANSWERS), F32),
+                jax.ShapeDtypeStruct((quest, 1), F32),
+            ),
+            in_specs=[vmem],
+            out_specs=(vmem, vmem, vmem),
+        )(packed)
         return tok, logp, loss.reshape(quest)
 
     return jax.shard_map(

time: 28.3 us -> 24.7 us (0.87)
  local copies, waits for them, and re-layouts: 2.39 us -> 0 us
  between operations: 2.4 us -> 0.64 us
  Pallas kernels: 23.3 us -> 23.8 us
    unnamed x2 -> x0, local copies, waits for them, and re-layouts: 2.39 us -> none
    pallas_call x1 -> x2, Pallas kernels: 23.3 us -> 23.8 us  [the longest x1 22.5 us: per_device(): pl.pallas_call(functools.partial(kernel, sizes), out_shape=jax.ShapeDtype...]
where the time goes in v2:
time: 24.7 us; the launch traced here: 24.4 us
  Pallas kernels  23.8 us (96%)
  between operations  0.64 us (3%)
    pallas_call x1, Pallas kernels, per_device(): pl.pallas_call(functools.partial(kernel, sizes), out_shape=jax.ShapeDtype...  22.5 us
    pallas_call x1, Pallas kernels, per_device(): pl.pallas_call(functools.partial(hand_out, conts, quest), out_shape=(jax....  1.26 us

profile of v2, /device:TPU:0, one launch (start us, length us, event | category | flops | bytes accessed | tf_op | source)
XLA Modules:
  0.0 24.4 jit_solution(15396178085770205926)
XLA Ops:
  0.6 22.5 %shard_map.112.packed_ref = f32[6,128]{1,0:T(8,128)} custom-call(s32[4]{0:T(128)} %qrow_ref.1, s32[4]{0:T(128)} %slot_ref.1, s32[4]{0:T(128)} %len_ref.1, s32[4]{0:T(128)} %gold_ref.1, bf16[4,2048,128]{2,1,0:T(8,128)(2,1)} %bitcast.5, bf16[4,256,128]{2,1,0:T(8,128)(2,1)} %bitcast.6, bf16[4,256,128]{2,1,0:T(8,128)(2,1)} %bitcast.7, ...), custom_call_target="tpu_custom_call" | custom-call | tf_op jit(solution)/shard_map/pallas_call | solution.py:295
  23.2 1.3 %shard_map.113 = (f32[4,128]{1,0:T(4,128)}, f32[1,4]{1,0:T(1,128)}, f32[1,1]{1,0:T(1,128)}) custom-call(f32[6,128]{1,0:T(8,128)} %shard_map.112.packed_ref), custom_call_target="tpu_custom_call" | custom-call | tf_op jit(solution)/shard_map/pallas_call | solution.py:329
